TPU v7x, 32 devices: a whole 2x2x4 slice. The times are simulated.
32 devices in a mesh: dom: 8 (over y, x, core), orb: 4 (over z).
Axes of the slice: x: 2, y: 2, z: 4, core: 2. Of those that a mesh axis runs over, the one named last changes fastest.
Arguments:
- orbitals: float32 [8, 64, 64, 128], P('orb', 'dom'), may hold values from -10.8 to 10.8
- initial_guess: float32 [8, 64, 64, 128], P('orb', 'dom'), may hold values from -350 to 350
- potential: float32 [64, 64, 128], P('dom'), may hold values from 0.1 to 2
- perturbation: float32 [64, 64, 128], P('dom'), may hold values from -6 to 6
- level_shifts: float32 [8], replicated, may hold values from 0.05 to 2
- assignment: int32 [8], P('orb'), may hold values from 0 to 7, each once
Outputs:
- updated_response: float32 [8, 64, 64, 128], P('orb', 'dom')
Inputs may be any that keep to these rules, and one draw needn't show every extreme that they name: `assignment`: every energy index appears in exactly one slot.
All inputs are finite; a program needn't handle non-finite values.
Results may differ from a plain program's by a relative error of at most 0.0003.
Values sent between devices are 32-bit elements; how exact they have to be, the bound alone decides.
No kernel may reach another device: no remote copies, remote signals or barrier semaphores. Data moves between devices by JAX's collectives and lax.ppermute only.
A program may use at most 128 MiB of HBM per device.

v0:
```python
import jax
import jax.numpy as jnp
from jax import lax
from jax.sharding import PartitionSpec as P

SWEEPS = 2
COARSE = 4
OMEGA = 0.8
KINETIC = 8.0


def with_halo(block, sides, width):
    for axis, dim in sides:
        count = lax.axis_size(axis)
        forward = [(i, i + 1) for i in range(count - 1)]
        forward.append((count - 1, 0))
        backward = [(target, source) for source, target in forward]
        low = lax.ppermute(
            lax.slice_in_dim(block, block.shape[dim] - width, None, axis=dim), axis, forward
        )
        high = lax.ppermute(lax.slice_in_dim(block, 0, width, axis=dim), axis, backward)
        block = jnp.concatenate([low, block, high], axis=dim)
    return block


def apply_level(field_values, potential_level, shift_column, level, padded):
    inverse_area = 0.25**level
    plus_x = padded[:, 2:]
    minus_x = padded[:, :-2]
    neighbours = (
        plus_x
        + minus_x
        + (jnp.roll(field_values, -1, 2) + jnp.roll(field_values, 1, 2))
        + (jnp.roll(field_values, -1, 3) + jnp.roll(field_values, 1, 3))
    )
    return (
        KINETIC * inverse_area * (6.0 * field_values - neighbours)
        + (potential_level + shift_column) * field_values
    )


def diagonal_of(potential_level, shift_column, level):
    return 6.0 * KINETIC * 0.25**level + potential_level + shift_column


def relax(estimate, source, potential_level, shift_column, level, padded):
    applied = apply_level(estimate, potential_level, shift_column, level, padded)
    return estimate + OMEGA * (source - applied) / diagonal_of(potential_level, shift_column, level)


def coarsen(field_values):
    lead, sx, sy, sz = field_values.shape
    return field_values.reshape(lead, sx // 2, 2, sy // 2, 2, sz // 2, 2).mean(axis=(2, 4, 6))


def refine(field_values):
    return jnp.repeat(jnp.repeat(jnp.repeat(field_values, 2, 1), 2, 2), 2, 3)


def fine_pad(field_values):
    return with_halo(field_values, (("dom", 1),), 1)


def middle_pad(field_values):
    return with_halo(field_values, (("dom", 1),), 1)


def on_device(orbitals, initial_guess, potential, perturbation, level_shifts, assignment):
    local_count = orbitals.shape[0]
    total_orbitals = level_shifts.shape[0]
    onehot = (assignment[:, None] == jnp.arange(total_orbitals, dtype=jnp.int32)[None, :]).astype(
        jnp.float32
    )
    shifts = jnp.sum(onehot * level_shifts[None, :], axis=1)
    shift_column = shifts[:, None, None, None]
    levels = [potential[None]]
    levels.append(coarsen(levels[0]))
    levels.append(coarsen(levels[1]))
    pads = [fine_pad, middle_pad]
    source = -(perturbation[None] * orbitals)
    sources = [
        source - apply_level(initial_guess, levels[0], shift_column, 0, fine_pad(initial_guess))
    ]
    estimates = []
    for level in range(2):
        current = sources[level]
        estimate = OMEGA * current / diagonal_of(levels[level], shift_column, level)
        estimate = relax(
            estimate, current, levels[level], shift_column, level, pads[level](estimate)
        )
        remainder = current - apply_level(
            estimate, levels[level], shift_column, level, pads[level](estimate)
        )
        estimates.append(estimate)
        sources.append(coarsen(remainder))
    lower = OMEGA * sources[2] / diagonal_of(levels[2], shift_column, 2)
    for sweep_index in range(COARSE - 1):
        padded = with_halo(lower, (("dom", 1),), 1)
        lower = relax(lower, sources[2], levels[2], shift_column, 2, padded)
    for level in (1, 0):
        estimate = estimates[level] + refine(lower)
        for sweep_index in range(SWEEPS):
            estimate = relax(
                estimate, sources[level], levels[level], shift_column, level, pads[level](estimate)
            )
        lower = estimate
    update = initial_guess + lower
    cells_total = orbitals.shape[1] * lax.axis_size("dom") * orbitals.shape[2] * orbitals.shape[3]
    everyone = lax.all_gather(orbitals, "orb", axis=0, tiled=True)
    flat_orbit = everyone.reshape(total_orbitals, -1)
    flat_update = update.reshape(local_count, -1)
    partial_intersection = jnp.einsum(
        "jc,ic->ji", flat_orbit, flat_update, precision=lax.Precision.HIGHEST
    )
    intersection = lax.psum(partial_intersection, "dom") / cells_total
    corrected = flat_update - jnp.einsum(
        "ji,jc->ic", intersection, flat_orbit, precision=lax.Precision.HIGHEST
    )
    result = corrected.reshape(update.shape)
    return result


def solution(mesh):
    in_specs = (
        P("orb", "dom", None, None),
        P("orb", "dom", None, None),
        P("dom", None, None),
        P("dom", None, None),
        P(),
        P("orb"),
    )
    out_specs = P("orb", "dom", None, None)
    return jax.shard_map(
        on_device, mesh=mesh, in_specs=in_specs, out_specs=out_specs, check_vma=False
    )
```

profile of v0, /device:TPU:0, one launch (start us, length us, event | category | flops | bytes accessed | tf_op | source)
XLA Modules:
  0.0 242.5 jit_solution(13926288601825531466)
XLA Ops:
  7.4 3.4 %collective-permute-start = (f32[2,1,64,128]{3,2,1,0:T(8,128)S(1)}, f32[2,1,64,128]{3,2,1,0:T(8,128)S(1)}, u32[]{:S(2)}, u32[]{:S(2)}) collective-permute-start(f32[2,1,64,128]{3,2,1,0:T(8,128)S(1)} %get-tuple-element.56), channel_id=1, source_target_pairs={{4,0},{8,4},{12,8},{16,12},{20,16},{24,20},{28,24},{0,28},{5,1},{9... | collective-permute-start | bytes 196616 | tf_op jit(solution)/shard_map/ppermute | solution.py:21
  10.9 1.4 copy.131
  12.3 1.6 fusion.137
  13.9 1.5 fusion.138
  17.7 18.1 %reshape_broadcast_in_dim.3 = f32[4,2,32,2,64,2]{5,4,3,2,1,0:T(8,128)} reshape(f32[8,64,128]{2,1,0:T(8,128)S(1)} %copy-done.9) | data formatting | bytes 524288 | tf_op jit(solution)/shard_map/reshape;broadcast_in_dim | solution.py:53
  37.4 1.4 copy.118
  39.8 7.1 %reduce_sum.47 = f32[4,32,64]{2,1,0:T(8,128)S(1)} reduce(f32[4,2,32,2,64,2]{5,4,3,2,1,0:T(8,128)} %reshape_broadcast_in_dim.3, f32[]{:T(128)} %constant.14.clone.1), dimensions={1,3,5}, to_apply=%region_2.0 | reduce | flops 57344 | bytes 294916 | tf_op jit(solution)/shard_map/reduce_sum | solution.py:53
  46.9 3.5 %div.73 = f32[2,2,16,2,32,2]{5,4,3,2,1,0:T(8,128)} reshape(f32[4,32,64]{2,1,0:T(8,128)S(1)} %get-tuple-element.99) | data formatting | bytes 65536 | tf_op jit(solution)/shard_map/div | solution.py:53
  50.4 1.8 reduce_sum.49
  53.0 1.8 pad_maximum_fusion.8
  54.8 2.3 copy.136
  57.1 1.4 copy.137
  58.6 4.9 %add_divide_fusion.3 = (f32[2,8,64,128]{2,1,3,0:T(8,128)S(1)}, f32[2,8,64,128]{2,1,3,0:T(8,128)S(1)}) fusion(f32[8,64,128]{1,0,2:T(8,128)S(1)} %copy.125, f32[2]{0:T(128)S(1)} %fusion.112, f32[2,8,64,128]{2,1,3,0:T(8,128)S(1)} %copy.131, f32[8,64,128]{1,0,2:T(8,128)S(1)} %copy.123, f32[2,8,64,127]{2,1,3,0:T(8,128)} %get-tuple-element.50, ...), kind=kLoop, calls=%fused_computation.9 | loop fusion | flops 2752512 | bytes 6029320 | tf_op jit(solution)/shard_map/div | solution.py:87
  64.4 2.7 %collective-permute-start.2 = (f32[2,1,64,128]{2,1,3,0:T(1,128)S(1)}, f32[2,1,64,128]{2,1,3,0:T(1,128)S(1)}, u32[]{:S(2)}, u32[]{:S(2)}) collective-permute-start(f32[2,1,64,128]{2,1,3,0:T(1,128)S(1)} %get-tuple-element.45), channel_id=1, source_target_pairs={{4,0},{8,4},{12,8},{16,12},{20,16},{24,20},{28,24},{0,28},{5,1},{9... | collective-permute-start | bytes 196616 | tf_op jit(solution)/shard_map/ppermute | solution.py:21
  67.1 2.5 %collective-permute-done.2 = f32[2,1,64,128]{2,1,3,0:T(1,128)S(1)} collective-permute-done((f32[2,1,64,128]{2,1,3,0:T(1,128)S(1)}, f32[2,1,64,128]{2,1,3,0:T(1,128)S(1)}, u32[]{:S(2)}, u32[]{:S(2)}) %collective-permute-start.2) | collective-permute-done | bytes 65568 | tf_op jit(solution)/shard_map/ppermute | solution.py:21
  69.7 2.8 %collective-permute-done.3 = f32[2,1,64,128]{2,1,3,0:T(1,128)S(1)} collective-permute-done((f32[2,1,64,128]{2,1,3,0:T(1,128)S(1)}, f32[2,1,64,128]{2,1,3,0:T(1,128)S(1)}, u32[]{:S(2)}, u32[]{:S(2)}) %collective-permute-start.3) | collective-permute-done | bytes 65568 | tf_op jit(solution)/shard_map/ppermute | solution.py:18
  72.4 1.4 fusion.10
  75.4 3.2 %collective-permute-done.4 = f32[2,1,64,128]{2,1,3,0:T(1,128)S(1)} collective-permute-done((f32[2,1,64,128]{2,1,3,0:T(1,128)S(1)}, f32[2,1,64,128]{2,1,3,0:T(1,128)S(1)}, u32[]{:S(2)}, u32[]{:S(2)}) %collective-permute-start.4) | collective-permute-done | bytes 65568 | tf_op jit(solution)/shard_map/ppermute | solution.py:21
  78.6 1.8 collective-permute-done.5
  80.4 2.2 fusion.20
  82.7 2.3 copy.126
  85.0 35.6 %reshape.71 = f32[2,4,2,32,2,64,2]{6,5,4,3,2,1,0:T(8,128)} reshape(f32[2,8,64,128]{3,2,1,0:T(8,128)} %copy.126) | data formatting | bytes 1048576 | tf_op jit(solution)/shard_map/reshape | solution.py:53
  120.6 12.2 %reduce_sum.46 = f32[2,4,32,64]{3,2,1,0:T(8,128)S(1)} reduce(f32[2,4,2,32,2,64,2]{6,5,4,3,2,1,0:T(8,128)} %reshape.71, f32[]{:T(128)} %constant.14.clone.1), dimensions={2,4,6}, to_apply=%region_1.0 | reduce | flops 114688 | bytes 589828 | tf_op jit(solution)/shard_map/reduce_sum | solution.py:53
  134.2 1.6 collective-permute-done.6
  135.8 2.6 %collective-permute-done.7 = f32[2,1,32,64]{3,2,1,0:T(8,128)S(1)} collective-permute-done((f32[2,1,32,64]{3,2,1,0:T(8,128)S(1)}, f32[2,1,32,64]{3,2,1,0:T(8,128)S(1)}, u32[]{:S(2)}, u32[]{:S(2)}) %collective-permute-start.7) | collective-permute-done | bytes 16416 | tf_op jit(solution)/shard_map/ppermute | solution.py:18
  141.2 2.7 %collective-permute-done.9 = f32[2,1,32,64]{3,2,1,0:T(8,128)S(1)} collective-permute-done((f32[2,1,32,64]{3,2,1,0:T(8,128)S(1)}, f32[2,1,32,64]{3,2,1,0:T(8,128)S(1)}, u32[]{:S(2)}, u32[]{:S(2)}) %collective-permute-start.9) | collective-permute-done | bytes 16416 | tf_op jit(solution)/shard_map/ppermute | solution.py:18
  144.7 6.5 %reshape.72 = f32[2,2,2,16,2,32,2]{6,5,4,3,2,1,0:T(8,128)} reshape(f32[2,4,32,64]{3,2,1,0:T(8,128)} %fusion.58) | data formatting | bytes 131072 | tf_op jit(solution)/shard_map/reshape | solution.py:53
  151.2 3.2 %reduce_sum.48 = f32[2,2,16,32]{3,2,1,0:T(8,128)} reduce(f32[2,2,2,16,2,32,2]{6,5,4,3,2,1,0:T(8,128)} %reshape.72, f32[]{:T(128)} %constant.14.clone.1), dimensions={2,4,6}, to_apply=%region_3.4 | reduce | flops 14336 | bytes 73732 | tf_op jit(solution)/shard_map/reduce_sum | solution.py:53
  157.1 2.6 %collective-permute-done.11 = f32[2,1,16,32]{3,2,1,0:T(8,128)S(1)} collective-permute-done((f32[2,1,16,32]{3,2,1,0:T(8,128)S(1)}, f32[2,1,16,32]{3,2,1,0:T(8,128)S(1)}, u32[]{:S(2)}, u32[]{:S(2)}) %collective-permute-start.11) | collective-permute-done | bytes 4128 | tf_op jit(solution)/shard_map/ppermute | solution.py:18
  162.3 2.7 %collective-permute-done.13 = f32[2,1,16,32]{3,2,1,0:T(8,128)S(1)} collective-permute-done((f32[2,1,16,32]{3,2,1,0:T(8,128)S(1)}, f32[2,1,16,32]{3,2,1,0:T(8,128)S(1)}, u32[]{:S(2)}, u32[]{:S(2)}) %collective-permute-start.13) | collective-permute-done | bytes 4128 | tf_op jit(solution)/shard_map/ppermute | solution.py:18
  167.5 2.7 %collective-permute-done.15 = f32[2,1,16,32]{3,2,1,0:T(8,128)S(1)} collective-permute-done((f32[2,1,16,32]{3,2,1,0:T(8,128)S(1)}, f32[2,1,16,32]{3,2,1,0:T(8,128)S(1)}, u32[]{:S(2)}, u32[]{:S(2)}) %collective-permute-start.15) | collective-permute-done | bytes 4128 | tf_op jit(solution)/shard_map/ppermute | solution.py:18
  171.0 1.6 copy.127
  172.7 1.7 broadcast_in_dim.26
  174.4 1.7 copy.128
  178.9 2.7 %collective-permute-done.17 = f32[2,1,32,64]{3,2,1,0:T(8,128)S(1)} collective-permute-done((f32[2,1,32,64]{3,2,1,0:T(8,128)S(1)}, f32[2,1,32,64]{3,2,1,0:T(8,128)S(1)}, u32[]{:S(2)}, u32[]{:S(2)}) %collective-permute-start.17) | collective-permute-done | bytes 16416 | tf_op jit(solution)/shard_map/ppermute | solution.py:18
  184.5 2.6 %collective-permute-done.19 = f32[2,1,32,64]{3,2,1,0:T(8,128)S(1)} collective-permute-done((f32[2,1,32,64]{3,2,1,0:T(8,128)S(1)}, f32[2,1,32,64]{3,2,1,0:T(8,128)S(1)}, u32[]{:S(2)}, u32[]{:S(2)}) %collective-permute-start.19) | collective-permute-done | bytes 16416 | tf_op jit(solution)/shard_map/ppermute | solution.py:18
  188.3 2.1 copy.130
  193.2 2.7 %collective-permute-done.20 = f32[2,1,64,128]{2,1,3,0:T(1,128)S(1)} collective-permute-done((f32[2,1,64,128]{2,1,3,0:T(1,128)S(1)}, f32[2,1,64,128]{2,1,3,0:T(1,128)S(1)}, u32[]{:S(2)}, u32[]{:S(2)}) %collective-permute-start.20) | collective-permute-done | bytes 65568 | tf_op jit(solution)/shard_map/ppermute | solution.py:21
  195.9 1.6 collective-permute-done.21
  197.5 1.4 fusion.11
  199.1 1.4 collective-permute-start.22
  201.4 2.0 collective-permute-done.22
  203.4 2.5 %collective-permute-done.23 = f32[2,1,64,128]{2,1,3,0:T(1,128)S(1)} collective-permute-done((f32[2,1,64,128]{2,1,3,0:T(1,128)S(1)}, f32[2,1,64,128]{2,1,3,0:T(1,128)S(1)}, u32[]{:S(2)}, u32[]{:S(2)}) %collective-permute-start.23) | collective-permute-done | bytes 65568 | tf_op jit(solution)/shard_map/ppermute | solution.py:18
  205.9 2.4 fusion.13
  208.2 2.4 %copy.133 = f32[2,8,64,128]{3,0,2,1:T(2,128)} copy(f32[2,8,64,128]{2,1,3,0:T(8,128)} %fusion.13) | data formatting | bytes 1048576 | tf_op jit(solution)/shard_map/add | solution.py:107
  210.7 6.7 %fusion.7 = f32[8,2]{0,1:T(2,128)S(1)} fusion(f32[2,8,64,128]{3,0,2,1:T(2,128)} %copy.133, f32[8,8,64,128]{3,2,1,0:T(8,128)} %all-gather.2.cloned.1.call-done), kind=kOutput, calls=%fused_computation.15 | convolution fusion | flops 12582912 | bytes 2621504 | tf_op jit(solution)/shard_map/jc,ic->ji/dot_general | solution.py:112
  218.6 12.1 %psum.7 = f32[8,2]{0,1:T(2,128)S(1)} all-reduce(f32[8,2]{0,1:T(2,128)S(1)} %fusion.7), channel_id=1, replica_groups=mesh['dom'=8,'orb'=4] {'dom'}, use_global_device_ids=true, to_apply=%region_5.6 | all-reduce | flops 16 | bytes 128 | tf_op jit(solution)/shard_map/psum | solution.py:115
  230.7 4.1 %fusion.4 = f32[1,2,512,128]{3,1,2,0:T(2,128)S(1)} fusion(f32[1,8,512,128]{3,2,1,0:T(8,128)S(1)} %bitcast.32, f32[1,2,512,128]{3,2,1,0:T(8,128)} %bitcast.34, f32[8,2]{0,1:T(2,128)S(1)} %psum.7), kind=kOutput, calls=%fused_computation.14 | convolution fusion | flops 12714000 | bytes 3145792 | tf_op jit(solution)/shard_map/ji,jc->ic/dot_general | solution.py:116
  (162 shorter events, 35.0 us)
Async XLA Ops:
  6.5 204.1 %all-gather.2.cloned.1.call-start = ((), (), s32[]{:S(2)}) async-start(), calls=%async_computation | async-start | bytes 2621440 | tf_op jit(solution)/shard_map/all_gather | solution.py:109
  7.4 45.6 %collective-permute-start = (f32[2,1,64,128]{3,2,1,0:T(8,128)S(1)}, f32[2,1,64,128]{3,2,1,0:T(8,128)S(1)}, u32[]{:S(2)}, u32[]{:S(2)}) collective-permute-start(f32[2,1,64,128]{3,2,1,0:T(8,128)S(1)} %get-tuple-element.56), channel_id=1, source_target_pairs={{4,0},{8,4},{12,8},{16,12},{20,16},{24,20},{28,24},{0,28},{5,1},{9... | collective-permute-start | bytes 196616 | tf_op jit(solution)/shard_map/ppermute | solution.py:21
  10.8 42.2 %collective-permute-start.1 = (f32[2,1,64,128]{3,2,1,0:T(8,128)S(1)}, f32[2,1,64,128]{3,2,1,0:T(8,128)}, u32[]{:S(2)}, u32[]{:S(2)}) collective-permute-start(f32[2,1,64,128]{3,2,1,0:T(8,128)S(1)} %get-tuple-element.55), channel_id=1, source_target_pairs={{0,4},{4,8},{8,12},{12,16},{16,20},{20,24},{24,28},{28,0},{1,5},{5... | collective-permute-start | bytes 196616 | tf_op jit(solution)/shard_map/ppermute | solution.py:18
  13.9 2.1 copy-start.9
  13.9 2.4 copy-start.8
  13.9 2.4 %copy-start.10 = (f32[2,8,64,128]{3,2,1,0:T(8,128)S(1)}, f32[2,8,64,128]{3,2,1,0:T(8,128)}, u32[]{:S(2)}) copy-start(f32[2,8,64,128]{3,2,1,0:T(8,128)} %param.6) | copy-start | bytes 1572868
  16.3 42.2 %copy-start = (f32[8,64,128]{1,0,2:T(8,128)}, f32[8,64,128]{1,0,2:T(8,128)S(1)}, u32[]{:S(2)}) copy-start(f32[8,64,128]{1,0,2:T(8,128)S(1)} %copy.123) | copy-start | bytes 786436
  35.7 3.0 %copy-start.12 = (f32[8,64,128]{2,1,0:T(8,128)S(1)}, f32[8,64,128]{2,1,0:T(8,128)}, u32[]{:S(2)}) copy-start(f32[8,64,128]{2,1,0:T(8,128)} %param.9) | copy-start | bytes 786436
  36.0 22.5 %copy-start.3 = (f32[8,64,128]{1,0,2:T(8,128)}, f32[8,64,128]{1,0,2:T(8,128)S(1)}, u32[]{:S(2)}) copy-start(f32[8,64,128]{1,0,2:T(8,128)S(1)} %copy.125) | copy-start | bytes 786436
  46.9 5.9 %copy-start.20 = (f32[8]{0:T(128)S(1)}, f32[8]{0:T(128)}, u32[]{:S(2)}) copy-start(f32[8]{0:T(128)} %param.10) | copy-start | bytes 100
  46.9 5.9 %copy-start.21 = (s32[2]{0:T(128)S(1)}, s32[2]{0:T(128)}, u32[]{:S(2)}) copy-start(s32[2]{0:T(128)} %param.11) | copy-start | bytes 28
  53.0 79.9 %copy-start.14 = (f32[2]{0:T(128)}, f32[2]{0:T(128)S(1)}, u32[]{:S(2)}) copy-start(f32[2]{0:T(128)S(1)} %fusion.112) | copy-start | bytes 28
  53.0 5.6 %copy-start.18 = (f32[2,8,64,1]{2,1,3,0:T(8,128)S(1)}, f32[2,8,64,1]{2,1,3,0:T(8,128)}, u32[]{:S(2)}) copy-start(f32[2,8,64,1]{2,1,3,0:T(8,128)} %get-tuple-element.51) | copy-start | bytes 12292
  53.0 5.6 %copy-start.19 = (f32[2,8,64,1]{2,1,3,0:T(8,128)S(1)}, f32[2,8,64,1]{2,1,3,0:T(8,128)}, u32[]{:S(2)}) copy-start(f32[2,8,64,1]{2,1,3,0:T(8,128)} %get-tuple-element.52) | copy-start | bytes 12292
  64.1 8.3 %copy-start.1 = (f32[8,64,128]{1,0,2:T(8,128)S(1)}, f32[8,64,128]{1,0,2:T(8,128)}, u32[]{:S(2)}) copy-start(f32[8,64,128]{1,0,2:T(8,128)} %copy-done) | copy-start | bytes 786436
  64.1 8.3 %copy-start.4 = (f32[8,64,128]{1,0,2:T(8,128)S(1)}, f32[8,64,128]{1,0,2:T(8,128)}, u32[]{:S(2)}) copy-start(f32[8,64,128]{1,0,2:T(8,128)} %copy-done.3) | copy-start | bytes 786436
  64.4 5.2 %collective-permute-start.2 = (f32[2,1,64,128]{2,1,3,0:T(1,128)S(1)}, f32[2,1,64,128]{2,1,3,0:T(1,128)S(1)}, u32[]{:S(2)}, u32[]{:S(2)}) collective-permute-start(f32[2,1,64,128]{2,1,3,0:T(1,128)S(1)} %get-tuple-element.45), channel_id=1, source_target_pairs={{4,0},{8,4},{12,8},{16,12},{20,16},{24,20},{28,24},{0,28},{5,1},{9... | collective-permute-start | bytes 196616 | tf_op jit(solution)/shard_map/ppermute | solution.py:21
  67.1 5.3 %collective-permute-start.3 = (f32[2,1,64,128]{2,1,3,0:T(1,128)S(1)}, f32[2,1,64,128]{2,1,3,0:T(1,128)S(1)}, u32[]{:S(2)}, u32[]{:S(2)}) collective-permute-start(f32[2,1,64,128]{2,1,3,0:T(1,128)S(1)} %get-tuple-element.46), channel_id=1, source_target_pairs={{0,4},{4,8},{8,12},{12,16},{16,20},{20,24},{24,28},{28,0},{1,5},{5... | collective-permute-start | bytes 196616 | tf_op jit(solution)/shard_map/ppermute | solution.py:18
  74.8 3.8 %collective-permute-start.4 = (f32[2,1,64,128]{2,1,3,0:T(1,128)S(1)}, f32[2,1,64,128]{2,1,3,0:T(1,128)S(1)}, u32[]{:S(2)}, u32[]{:S(2)}) collective-permute-start(f32[2,1,64,128]{2,1,3,0:T(1,128)S(1)} %get-tuple-element.35), channel_id=1, source_target_pairs={{4,0},{8,4},{12,8},{16,12},{20,16},{24,20},{28,24},{0,28},{5,1},{9... | collective-permute-start | bytes 196616 | tf_op jit(solution)/shard_map/ppermute | solution.py:21
  74.9 5.5 %collective-permute-start.5 = (f32[2,1,64,128]{2,1,3,0:T(1,128)S(1)}, f32[2,1,64,128]{2,1,3,0:T(1,128)S(1)}, u32[]{:S(2)}, u32[]{:S(2)}) collective-permute-start(f32[2,1,64,128]{2,1,3,0:T(1,128)S(1)} %get-tuple-element.36), channel_id=1, source_target_pairs={{0,4},{4,8},{8,12},{12,16},{16,20},{20,24},{24,28},{28,0},{1,5},{5... | collective-permute-start | bytes 196616 | tf_op jit(solution)/shard_map/ppermute | solution.py:18
  133.0 10.8 %copy-start.15 = (f32[2]{0:T(128)S(1)}, f32[2]{0:T(128)}, u32[]{:S(2)}) copy-start(f32[2]{0:T(128)} %copy-done.14) | copy-start | bytes 28
  133.2 2.6 %collective-permute-start.6 = (f32[2,1,32,64]{3,2,1,0:T(8,128)S(1)}, f32[2,1,32,64]{3,2,1,0:T(8,128)S(1)}, u32[]{:S(2)}, u32[]{:S(2)}) collective-permute-start(f32[2,1,32,64]{3,2,1,0:T(8,128)S(1)} %get-tuple-element.97), channel_id=1, source_target_pairs={{4,0},{8,4},{12,8},{16,12},{20,16},{24,20},{28,24},{0,28},{5,1},{9... | collective-permute-start | bytes 49160 | tf_op jit(solution)/shard_map/ppermute | solution.py:21
  134.2 4.2 %collective-permute-start.7 = (f32[2,1,32,64]{3,2,1,0:T(8,128)S(1)}, f32[2,1,32,64]{3,2,1,0:T(8,128)S(1)}, u32[]{:S(2)}, u32[]{:S(2)}) collective-permute-start(f32[2,1,32,64]{3,2,1,0:T(8,128)S(1)} %get-tuple-element.98), channel_id=1, source_target_pairs={{0,4},{4,8},{8,12},{12,16},{16,20},{20,24},{24,28},{28,0},{1,5},{5... | collective-permute-start | bytes 49160 | tf_op jit(solution)/shard_map/ppermute | solution.py:18
  139.5 1.7 collective-permute-start.8
  139.6 4.3 %collective-permute-start.9 = (f32[2,1,32,64]{3,2,1,0:T(8,128)S(1)}, f32[2,1,32,64]{3,2,1,0:T(8,128)S(1)}, u32[]{:S(2)}, u32[]{:S(2)}) collective-permute-start(f32[2,1,32,64]{3,2,1,0:T(8,128)S(1)} %get-tuple-element.88), channel_id=1, source_target_pairs={{0,4},{4,8},{8,12},{12,16},{16,20},{20,24},{24,28},{28,0},{1,5},{5... | collective-permute-start | bytes 49160 | tf_op jit(solution)/shard_map/ppermute | solution.py:18
  154.4 15.8 %copy-start.11 = (f32[2,2,16,32]{3,2,1,0:T(8,128)S(1)}, f32[2,2,16,32]{3,2,1,0:T(8,128)}, u32[]{:S(2)}) copy-start(f32[2,2,16,32]{3,2,1,0:T(8,128)} %reduce_sum.48) | copy-start | bytes 24580
  154.4 15.8 %copy-start.13 = (f32[2,16,32]{2,1,0:T(8,128)S(1)}, f32[2,16,32]{2,1,0:T(8,128)}, u32[]{:S(2)}) copy-start(f32[2,16,32]{2,1,0:T(8,128)} %get-tuple-element.131) | copy-start | bytes 12292
  154.4 15.8 %copy-start.16 = (f32[2]{0:T(128)S(1)}, f32[2]{0:T(128)}, u32[]{:S(2)}) copy-start(f32[2]{0:T(128)} %copy-done.14) | copy-start | bytes 28
  155.5 1.6 collective-permute-start.10
  155.6 4.1 %collective-permute-start.11 = (f32[2,1,16,32]{3,2,1,0:T(8,128)S(1)}, f32[2,1,16,32]{3,2,1,0:T(8,128)S(1)}, u32[]{:S(2)}, u32[]{:S(2)}) collective-permute-start(f32[2,1,16,32]{3,2,1,0:T(8,128)S(1)} %get-tuple-element.130), channel_id=1, source_target_pairs={{0,4},{4,8},{8,12},{12,16},{16,20},{20,24},{24,28},{28,0},{1,5},{5... | collective-permute-start | bytes 12296 | tf_op jit(solution)/shard_map/ppermute | solution.py:18
  160.8 1.5 collective-permute-start.12
  160.8 4.1 %collective-permute-start.13 = (f32[2,1,16,32]{3,2,1,0:T(8,128)S(1)}, f32[2,1,16,32]{3,2,1,0:T(8,128)S(1)}, u32[]{:S(2)}, u32[]{:S(2)}) collective-permute-start(f32[2,1,16,32]{3,2,1,0:T(8,128)S(1)} %get-tuple-element.120), channel_id=1, source_target_pairs={{0,4},{4,8},{8,12},{12,16},{16,20},{20,24},{24,28},{28,0},{1,5},{5... | collective-permute-start | bytes 12296 | tf_op jit(solution)/shard_map/ppermute | solution.py:18
  166.0 1.5 collective-permute-start.14
  166.1 4.1 %collective-permute-start.15 = (f32[2,1,16,32]{3,2,1,0:T(8,128)S(1)}, f32[2,1,16,32]{3,2,1,0:T(8,128)S(1)}, u32[]{:S(2)}, u32[]{:S(2)}) collective-permute-start(f32[2,1,16,32]{3,2,1,0:T(8,128)S(1)} %get-tuple-element.110), channel_id=1, source_target_pairs={{0,4},{4,8},{8,12},{12,16},{16,20},{20,24},{24,28},{28,0},{1,5},{5... | collective-permute-start | bytes 12296 | tf_op jit(solution)/shard_map/ppermute | solution.py:18
  177.1 10.0 %copy-start.17 = (f32[2]{0:T(128)S(1)}, f32[2]{0:T(128)}, u32[]{:S(2)}) copy-start(f32[2]{0:T(128)} %copy-done.14) | copy-start | bytes 28
  177.3 1.7 collective-permute-start.16
  177.3 4.3 %collective-permute-start.17 = (f32[2,1,32,64]{3,2,1,0:T(8,128)S(1)}, f32[2,1,32,64]{3,2,1,0:T(8,128)S(1)}, u32[]{:S(2)}, u32[]{:S(2)}) collective-permute-start(f32[2,1,32,64]{3,2,1,0:T(8,128)S(1)} %get-tuple-element.78), channel_id=1, source_target_pairs={{0,4},{4,8},{8,12},{12,16},{16,20},{20,24},{24,28},{28,0},{1,5},{5... | collective-permute-start | bytes 49160 | tf_op jit(solution)/shard_map/ppermute | solution.py:18
  182.7 1.8 collective-permute-start.18
  182.9 4.2 %collective-permute-start.19 = (f32[2,1,32,64]{3,2,1,0:T(8,128)S(1)}, f32[2,1,32,64]{3,2,1,0:T(8,128)S(1)}, u32[]{:S(2)}, u32[]{:S(2)}) collective-permute-start(f32[2,1,32,64]{3,2,1,0:T(8,128)S(1)} %get-tuple-element.68), channel_id=1, source_target_pairs={{0,4},{4,8},{8,12},{12,16},{16,20},{20,24},{24,28},{28,0},{1,5},{5... | collective-permute-start | bytes 49160 | tf_op jit(solution)/shard_map/ppermute | solution.py:18
  192.1 3.8 %collective-permute-start.20 = (f32[2,1,64,128]{2,1,3,0:T(1,128)S(1)}, f32[2,1,64,128]{2,1,3,0:T(1,128)S(1)}, u32[]{:S(2)}, u32[]{:S(2)}) collective-permute-start(f32[2,1,64,128]{2,1,3,0:T(1,128)S(1)} %get-tuple-element.25), channel_id=1, source_target_pairs={{4,0},{8,4},{12,8},{16,12},{20,16},{24,20},{28,24},{0,28},{5,1},{9... | collective-permute-start | bytes 196616 | tf_op jit(solution)/shard_map/ppermute | solution.py:21
  192.2 5.3 %collective-permute-start.21 = (f32[2,1,64,128]{2,1,3,0:T(1,128)S(1)}, f32[2,1,64,128]{2,1,3,0:T(1,128)S(1)}, u32[]{:S(2)}, u32[]{:S(2)}) collective-permute-start(f32[2,1,64,128]{2,1,3,0:T(1,128)S(1)} %get-tuple-element.26), channel_id=1, source_target_pairs={{0,4},{4,8},{8,12},{12,16},{16,20},{20,24},{24,28},{28,0},{1,5},{5... | collective-permute-start | bytes 196616 | tf_op jit(solution)/shard_map/ppermute | solution.py:18
  192.8 4.7 %copy-start.2 = (f32[8,64,128]{1,0,2:T(8,128)S(1)}, f32[8,64,128]{1,0,2:T(8,128)}, u32[]{:S(2)}) copy-start(f32[8,64,128]{1,0,2:T(8,128)} %copy-done) | copy-start | bytes 786436
  192.8 4.7 %copy-start.5 = (f32[8,64,128]{1,0,2:T(8,128)S(1)}, f32[8,64,128]{1,0,2:T(8,128)}, u32[]{:S(2)}) copy-start(f32[8,64,128]{1,0,2:T(8,128)} %copy-done.3) | copy-start | bytes 786436
  199.1 4.2 %collective-permute-start.22 = (f32[2,1,64,128]{2,1,3,0:T(1,128)S(1)}, f32[2,1,64,128]{2,1,3,0:T(1,128)S(1)}, u32[]{:S(2)}, u32[]{:S(2)}) collective-permute-start(f32[2,1,64,128]{2,1,3,0:T(1,128)S(1)} %get-tuple-element.15), channel_id=1, source_target_pairs={{4,0},{8,4},{12,8},{16,12},{20,16},{24,20},{28,24},{0,28},{5,1},{9... | collective-permute-start | bytes 196616 | tf_op jit(solution)/shard_map/ppermute | solution.py:21
  200.6 5.3 %collective-permute-start.23 = (f32[2,1,64,128]{2,1,3,0:T(1,128)S(1)}, f32[2,1,64,128]{2,1,3,0:T(1,128)S(1)}, u32[]{:S(2)}, u32[]{:S(2)}) collective-permute-start(f32[2,1,64,128]{2,1,3,0:T(1,128)S(1)} %get-tuple-element.16), channel_id=1, source_target_pairs={{0,4},{4,8},{8,12},{12,16},{16,20},{20,24},{24,28},{28,0},{1,5},{5... | collective-permute-start | bytes 196616 | tf_op jit(solution)/shard_map/ppermute | solution.py:18
  208.2 9.2 %copy-start.6 = (f32[2,8,64,128]{2,1,3,0:T(8,128)S(1)}, f32[2,8,64,128]{2,1,3,0:T(8,128)}, u32[]{:S(2)}) copy-start(f32[2,8,64,128]{2,1,3,0:T(8,128)} %fusion.13) | copy-start | bytes 1572868
  210.7 20.0 %copy-start.7 = (f32[8,8,64,128]{3,2,1,0:T(8,128)S(1)}, f32[8,8,64,128]{3,2,1,0:T(8,128)}, u32[]{:S(2)}) copy-start(f32[8,8,64,128]{3,2,1,0:T(8,128)} %all-gather.2.cloned.1.call-done) | copy-start | bytes 6291460
Sparse Core Ops, SparseCore 0:
  11.0 47.1 all-gather.1
where the time goes:
time: 244 us; the launch traced here: 242 us
  local copies, waits for them, and re-layouts  101 us (41%)
  other arithmetic  45.7 us (19%)
  waiting for transfers between devices  45.6 us (19%)
  between operations  14 us (6%)
  starting transfers between devices  13.1 us (5%)
  blocking collectives  12.1 us (5%)
  matrix products  10.9 us (4%)
    reshape x2, local copies, waits for them, and re-layouts, coarsen(): field_values.reshape(lead, sx // 2, 2, sy // 2, 2, sz // 2, 2)  42.1 us
    ppermute x12, waiting for transfers between devices, with_halo(): lax.ppermute(lax.slice_in_dim(block, block.shape[dim] - width, None, axis...  27.4 us
    reduce_sum x4, other arithmetic, coarsen(): field_values.reshape(lead, sx // 2, 2, sy // 2, 2, sz // 2, 2)  24.3 us
    ppermute x12, waiting for transfers between devices, with_halo(): lax.ppermute(lax.slice_in_dim(block, 0, width, axis=dim), axis, backward)  18.2 us
    another operation x1, local copies, waits for them, and re-layouts, coarsen(): field_values.reshape(lead, sx // 2, 2, sy // 2, 2, sz // 2, 2)  18.1 us
    psum x1, blocking collectives, on_device(): intersection = lax.psum(partial_intersection, 'dom') / cells_total  12.1 us
    ppermute x12, starting transfers between devices, with_halo(): lax.ppermute(lax.slice_in_dim(block, 0, width, axis=dim), axis, backward)  9.35 us
    unnamed x51, local copies, waits for them, and re-layouts  8.67 us
  transfers between devices with their start and end apart: 25, of which 22 were waited for; matrix products, arithmetic and copies ran while one was open for 59% of the time, Pallas kernels for 0%

commit v1 on v0

--- a/solution.py
+++ b/solution.py
@@ -112,7 +112,12 @@
     partial_intersection = jnp.einsum(
         "jc,ic->ji", flat_orbit, flat_update, precision=lax.Precision.HIGHEST
     )
-    intersection = lax.psum(partial_intersection, "dom") / cells_total
+
+    def push_the_rings(my_data, a_name):
+        z = jnp.sum(lax.all_gather(my_data, a_name), axis=0)
+        return z
+
+    intersection = push_the_rings(partial_intersection, "dom") / cells_total
     corrected = flat_update - jnp.einsum(
         "ji,jc->ic", intersection, flat_orbit, precision=lax.Precision.HIGHEST
     )

time: 244 us -> 237 us (0.971)
  blocking collectives: 12.1 us -> 7.94 us
    psum x1 -> x0, blocking collectives: 12.1 us -> none  [on_device(): intersection = lax.psum(partial_intersection, 'dom') / cells_total]
    all_gather x0 -> x1, blocking collectives: none -> 7.94 us  [push_the_rings(): z = jnp.sum(lax.all_gather(my_data, a_name), axis=0)]
  transfers between devices with their start and end apart: 25 -> 25, of which waited for: 22 -> 22; matrix products, arithmetic and copies ran while one was open for 59% -> 61% of each run, Pallas kernels for 0% -> 0%
where the time goes in v1:
time: 237 us; the launch traced here: 236 us
  local copies, waits for them, and re-layouts  99.5 us (42%)
  waiting for transfers between devices  45.7 us (19%)
  other arithmetic  45.7 us (19%)
  between operations  14 us (6%)
  starting transfers between devices  13.1 us (6%)
  matrix products  9.7 us (4%)
  blocking collectives  7.94 us (3%)
    reshape x2, local copies, waits for them, and re-layouts, coarsen(): field_values.reshape(lead, sx // 2, 2, sy // 2, 2, sz // 2, 2)  42.1 us
    ppermute x12, waiting for transfers between devices, with_halo(): lax.ppermute(lax.slice_in_dim(block, block.shape[dim] - width, None, axis...  27.4 us
    reduce_sum x4, other arithmetic, coarsen(): field_values.reshape(lead, sx // 2, 2, sy // 2, 2, sz // 2, 2)  24.3 us
    ppermute x12, waiting for transfers between devices, with_halo(): lax.ppermute(lax.slice_in_dim(block, 0, width, axis=dim), axis, backward)  18.2 us
    another operation x1, local copies, waits for them, and re-layouts, coarsen(): field_values.reshape(lead, sx // 2, 2, sy // 2, 2, sz // 2, 2)  18.1 us
    ppermute x12, starting transfers between devices, with_halo(): lax.ppermute(lax.slice_in_dim(block, 0, width, axis=dim), axis, backward)  9.35 us
    unnamed x51, local copies, waits for them, and re-layouts  8.67 us
    all_gather x1, blocking collectives, push_the_rings(): z = jnp.sum(lax.all_gather(my_data, a_name), axis=0)  7.94 us
  transfers between devices with their start and end apart: 25, of which 22 were waited for; matrix products, arithmetic and copies ran while one was open for 61% of the time, Pallas kernels for 0%

profile of v1, /device:TPU:0, one launch (start us, length us, event | category | flops | bytes accessed | tf_op | source)
XLA Modules:
  0.0 235.7 jit_solution(14274011410103325921)
XLA Ops:
  7.4 3.4 %collective-permute-start = (f32[2,1,64,128]{3,2,1,0:T(8,128)S(1)}, f32[2,1,64,128]{3,2,1,0:T(8,128)S(1)}, u32[]{:S(2)}, u32[]{:S(2)}) collective-permute-start(f32[2,1,64,128]{3,2,1,0:T(8,128)S(1)} %get-tuple-element.56), channel_id=1, source_target_pairs={{4,0},{8,4},{12,8},{16,12},{20,16},{24,20},{28,24},{0,28},{5,1},{9... | collective-permute-start | bytes 196616 | tf_op jit(solution)/shard_map/ppermute | solution.py:21
  10.9 1.4 copy.135
  12.3 1.6 fusion.137
  13.9 1.5 fusion.138
  17.7 18.1 %reshape_broadcast_in_dim.3 = f32[4,2,32,2,64,2]{5,4,3,2,1,0:T(8,128)} reshape(f32[8,64,128]{2,1,0:T(8,128)S(1)} %copy-done.9) | data formatting | bytes 524288 | tf_op jit(solution)/shard_map/reshape;broadcast_in_dim | solution.py:53
  37.4 1.4 copy.122
  39.8 7.1 %reduce_sum.56 = f32[4,32,64]{2,1,0:T(8,128)S(1)} reduce(f32[4,2,32,2,64,2]{5,4,3,2,1,0:T(8,128)} %reshape_broadcast_in_dim.3, f32[]{:T(128)} %constant.14.clone.1), dimensions={1,3,5}, to_apply=%region_2.0 | reduce | flops 57344 | bytes 294916 | tf_op jit(solution)/shard_map/reduce_sum | solution.py:53
  46.9 3.5 %div.73 = f32[2,2,16,2,32,2]{5,4,3,2,1,0:T(8,128)} reshape(f32[4,32,64]{2,1,0:T(8,128)S(1)} %get-tuple-element.99) | data formatting | bytes 65536 | tf_op jit(solution)/shard_map/div | solution.py:53
  50.4 1.8 reduce_sum.58
  53.0 1.8 pad_maximum_fusion.8
  54.8 2.3 copy.140
  57.1 1.4 copy.141
  58.6 4.9 %add_divide_fusion.3 = (f32[2,8,64,128]{2,1,3,0:T(8,128)S(1)}, f32[2,8,64,128]{2,1,3,0:T(8,128)S(1)}) fusion(f32[8,64,128]{1,0,2:T(8,128)S(1)} %copy.129, f32[2]{0:T(128)S(1)} %fusion.112, f32[2,8,64,128]{2,1,3,0:T(8,128)S(1)} %copy.135, f32[8,64,128]{1,0,2:T(8,128)S(1)} %copy.127, f32[2,8,64,127]{2,1,3,0:T(8,128)} %get-tuple-element.50, ...), kind=kLoop, calls=%fused_computation.9 | loop fusion | flops 2752512 | bytes 6029320 | tf_op jit(solution)/shard_map/div | solution.py:87
  64.4 2.7 %collective-permute-start.2 = (f32[2,1,64,128]{2,1,3,0:T(1,128)S(1)}, f32[2,1,64,128]{2,1,3,0:T(1,128)S(1)}, u32[]{:S(2)}, u32[]{:S(2)}) collective-permute-start(f32[2,1,64,128]{2,1,3,0:T(1,128)S(1)} %get-tuple-element.45), channel_id=1, source_target_pairs={{4,0},{8,4},{12,8},{16,12},{20,16},{24,20},{28,24},{0,28},{5,1},{9... | collective-permute-start | bytes 196616 | tf_op jit(solution)/shard_map/ppermute | solution.py:21
  67.1 2.5 %collective-permute-done.2 = f32[2,1,64,128]{2,1,3,0:T(1,128)S(1)} collective-permute-done((f32[2,1,64,128]{2,1,3,0:T(1,128)S(1)}, f32[2,1,64,128]{2,1,3,0:T(1,128)S(1)}, u32[]{:S(2)}, u32[]{:S(2)}) %collective-permute-start.2) | collective-permute-done | bytes 65568 | tf_op jit(solution)/shard_map/ppermute | solution.py:21
  69.7 2.8 %collective-permute-done.3 = f32[2,1,64,128]{2,1,3,0:T(1,128)S(1)} collective-permute-done((f32[2,1,64,128]{2,1,3,0:T(1,128)S(1)}, f32[2,1,64,128]{2,1,3,0:T(1,128)S(1)}, u32[]{:S(2)}, u32[]{:S(2)}) %collective-permute-start.3) | collective-permute-done | bytes 65568 | tf_op jit(solution)/shard_map/ppermute | solution.py:18
  72.4 1.4 fusion.10
  75.4 3.2 %collective-permute-done.4 = f32[2,1,64,128]{2,1,3,0:T(1,128)S(1)} collective-permute-done((f32[2,1,64,128]{2,1,3,0:T(1,128)S(1)}, f32[2,1,64,128]{2,1,3,0:T(1,128)S(1)}, u32[]{:S(2)}, u32[]{:S(2)}) %collective-permute-start.4) | collective-permute-done | bytes 65568 | tf_op jit(solution)/shard_map/ppermute | solution.py:21
  78.6 1.8 collective-permute-done.5
  80.4 2.2 fusion.20
  82.7 2.3 copy.130
  85.0 35.6 %reshape.71 = f32[2,4,2,32,2,64,2]{6,5,4,3,2,1,0:T(8,128)} reshape(f32[2,8,64,128]{3,2,1,0:T(8,128)} %copy.130) | data formatting | bytes 1048576 | tf_op jit(solution)/shard_map/reshape | solution.py:53
  120.6 12.2 %reduce_sum.55 = f32[2,4,32,64]{3,2,1,0:T(8,128)S(1)} reduce(f32[2,4,2,32,2,64,2]{6,5,4,3,2,1,0:T(8,128)} %reshape.71, f32[]{:T(128)} %constant.14.clone.1), dimensions={2,4,6}, to_apply=%region_1.0 | reduce | flops 114688 | bytes 589828 | tf_op jit(solution)/shard_map/reduce_sum | solution.py:53
  134.2 1.6 collective-permute-done.6
  135.8 2.6 %collective-permute-done.7 = f32[2,1,32,64]{3,2,1,0:T(8,128)S(1)} collective-permute-done((f32[2,1,32,64]{3,2,1,0:T(8,128)S(1)}, f32[2,1,32,64]{3,2,1,0:T(8,128)S(1)}, u32[]{:S(2)}, u32[]{:S(2)}) %collective-permute-start.7) | collective-permute-done | bytes 16416 | tf_op jit(solution)/shard_map/ppermute | solution.py:18
  141.2 2.7 %collective-permute-done.9 = f32[2,1,32,64]{3,2,1,0:T(8,128)S(1)} collective-permute-done((f32[2,1,32,64]{3,2,1,0:T(8,128)S(1)}, f32[2,1,32,64]{3,2,1,0:T(8,128)S(1)}, u32[]{:S(2)}, u32[]{:S(2)}) %collective-permute-start.9) | collective-permute-done | bytes 16416 | tf_op jit(solution)/shard_map/ppermute | solution.py:18
  144.7 6.5 %reshape.72 = f32[2,2,2,16,2,32,2]{6,5,4,3,2,1,0:T(8,128)} reshape(f32[2,4,32,64]{3,2,1,0:T(8,128)} %fusion.58) | data formatting | bytes 131072 | tf_op jit(solution)/shard_map/reshape | solution.py:53
  151.2 3.2 %reduce_sum.57 = f32[2,2,16,32]{3,2,1,0:T(8,128)} reduce(f32[2,2,2,16,2,32,2]{6,5,4,3,2,1,0:T(8,128)} %reshape.72, f32[]{:T(128)} %constant.14.clone.1), dimensions={2,4,6}, to_apply=%region_3.4 | reduce | flops 14336 | bytes 73732 | tf_op jit(solution)/shard_map/reduce_sum | solution.py:53
  157.1 2.6 %collective-permute-done.11 = f32[2,1,16,32]{3,2,1,0:T(8,128)S(1)} collective-permute-done((f32[2,1,16,32]{3,2,1,0:T(8,128)S(1)}, f32[2,1,16,32]{3,2,1,0:T(8,128)S(1)}, u32[]{:S(2)}, u32[]{:S(2)}) %collective-permute-start.11) | collective-permute-done | bytes 4128 | tf_op jit(solution)/shard_map/ppermute | solution.py:18
  162.3 2.7 %collective-permute-done.13 = f32[2,1,16,32]{3,2,1,0:T(8,128)S(1)} collective-permute-done((f32[2,1,16,32]{3,2,1,0:T(8,128)S(1)}, f32[2,1,16,32]{3,2,1,0:T(8,128)S(1)}, u32[]{:S(2)}, u32[]{:S(2)}) %collective-permute-start.13) | collective-permute-done | bytes 4128 | tf_op jit(solution)/shard_map/ppermute | solution.py:18
  167.5 2.7 %collective-permute-done.15 = f32[2,1,16,32]{3,2,1,0:T(8,128)S(1)} collective-permute-done((f32[2,1,16,32]{3,2,1,0:T(8,128)S(1)}, f32[2,1,16,32]{3,2,1,0:T(8,128)S(1)}, u32[]{:S(2)}, u32[]{:S(2)}) %collective-permute-start.15) | collective-permute-done | bytes 4128 | tf_op jit(solution)/shard_map/ppermute | solution.py:18
  171.0 1.6 copy.131
  172.7 1.7 broadcast_in_dim.26
  174.4 1.7 copy.132
  178.9 2.7 %collective-permute-done.17 = f32[2,1,32,64]{3,2,1,0:T(8,128)S(1)} collective-permute-done((f32[2,1,32,64]{3,2,1,0:T(8,128)S(1)}, f32[2,1,32,64]{3,2,1,0:T(8,128)S(1)}, u32[]{:S(2)}, u32[]{:S(2)}) %collective-permute-start.17) | collective-permute-done | bytes 16416 | tf_op jit(solution)/shard_map/ppermute | solution.py:18
  184.5 2.6 %collective-permute-done.19 = f32[2,1,32,64]{3,2,1,0:T(8,128)S(1)} collective-permute-done((f32[2,1,32,64]{3,2,1,0:T(8,128)S(1)}, f32[2,1,32,64]{3,2,1,0:T(8,128)S(1)}, u32[]{:S(2)}, u32[]{:S(2)}) %collective-permute-start.19) | collective-permute-done | bytes 16416 | tf_op jit(solution)/shard_map/ppermute | solution.py:18
  188.3 2.1 copy.134
  193.2 2.7 %collective-permute-done.20 = f32[2,1,64,128]{2,1,3,0:T(1,128)S(1)} collective-permute-done((f32[2,1,64,128]{2,1,3,0:T(1,128)S(1)}, f32[2,1,64,128]{2,1,3,0:T(1,128)S(1)}, u32[]{:S(2)}, u32[]{:S(2)}) %collective-permute-start.20) | collective-permute-done | bytes 65568 | tf_op jit(solution)/shard_map/ppermute | solution.py:21
  195.9 1.6 collective-permute-done.21
  197.5 1.4 fusion.11
  199.1 1.4 collective-permute-start.22
  201.4 2.0 collective-permute-done.22
  203.4 2.5 %collective-permute-done.23 = f32[2,1,64,128]{2,1,3,0:T(1,128)S(1)} collective-permute-done((f32[2,1,64,128]{2,1,3,0:T(1,128)S(1)}, f32[2,1,64,128]{2,1,3,0:T(1,128)S(1)}, u32[]{:S(2)}, u32[]{:S(2)}) %collective-permute-start.23) | collective-permute-done | bytes 65568 | tf_op jit(solution)/shard_map/ppermute | solution.py:18
  205.9 2.4 %fusion.13 = f32[2,8,64,128]{2,1,3,0:T(8,128)} fusion(f32[2,8,64,128]{2,1,3,0:T(8,128)S(1)} %copy.135, f32[2,8,64,128]{2,1,3,0:T(8,128)S(1)} %fusion.11, f32[2,8,64,128]{2,1,3,0:T(8,128)S(1)} %get-tuple-element.6, f32[2,1,64,128]{2,1,3,0:T(1,128)S(1)} %collective-permute-done.23, f32[2,1,64,128]{2,1,3,0:T(1,128)S(1)} %collective-permute-done.22, ...), kind=kLoop, calls=%fused_computation.19 | loop fusion | flops 3014656 | bytes 4849672 | tf_op jit(solution)/shard_map/add | solution.py:107
  208.2 1.7 copy.137
  210.3 6.6 %fusion.7 = f32[1,8,2]{1,2,0:T(2,128)S(1)} fusion(f32[2,8,64,128]{3,0,2,1:T(2,128)S(1)} %copy.137, f32[8,8,64,128]{3,2,1,0:T(8,128)} %all-gather.4.cloned.1.call-done), kind=kOutput, calls=%fused_computation.15 | convolution fusion | flops 12582912 | bytes 2621504 | tf_op jit(solution)/shard_map/jc,ic->ji/dot_general | solution.py:112
  216.9 7.9 %all-gather.1 = f32[8,8,2]{1,2,0:T(2,128)S(1)} all-gather(f32[1,8,2]{1,2,0:T(2,128)S(1)} %fusion.7), channel_id=2, replica_groups=mesh['dom'=8,'orb'=4] {'dom'}, dimensions={0}, use_global_device_ids=true | all-gather | bytes 576 | tf_op jit(solution)/shard_map/all_gather | solution.py:117
  224.9 3.1 %fusion.4 = f32[1,2,512,128]{3,1,2,0:T(2,128)S(1)} fusion(f32[1,8,512,128]{3,2,1,0:T(8,128)S(1)} %bitcast.34, f32[1,2,512,128]{3,2,1,0:T(8,128)S(1)} %bitcast.36, f32[8,2]{0,1:T(2,128)S(1)} %reduce_sum.59), kind=kOutput, calls=%fused_computation.14 | convolution fusion | flops 12714000 | bytes 3145792 | tf_op jit(solution)/shard_map/ji,jc->ic/dot_general | solution.py:121
  (163 shorter events, 34.2 us)
Async XLA Ops:
  6.5 203.8 %all-gather.4.cloned.1.call-start = ((), (), s32[]{:S(2)}) async-start(), calls=%async_computation | async-start | bytes 2621440 | tf_op jit(solution)/shard_map/all_gather | solution.py:109
  7.4 45.6 %collective-permute-start = (f32[2,1,64,128]{3,2,1,0:T(8,128)S(1)}, f32[2,1,64,128]{3,2,1,0:T(8,128)S(1)}, u32[]{:S(2)}, u32[]{:S(2)}) collective-permute-start(f32[2,1,64,128]{3,2,1,0:T(8,128)S(1)} %get-tuple-element.56), channel_id=1, source_target_pairs={{4,0},{8,4},{12,8},{16,12},{20,16},{24,20},{28,24},{0,28},{5,1},{9... | collective-permute-start | bytes 196616 | tf_op jit(solution)/shard_map/ppermute | solution.py:21
  10.8 42.2 %collective-permute-start.1 = (f32[2,1,64,128]{3,2,1,0:T(8,128)S(1)}, f32[2,1,64,128]{3,2,1,0:T(8,128)}, u32[]{:S(2)}, u32[]{:S(2)}) collective-permute-start(f32[2,1,64,128]{3,2,1,0:T(8,128)S(1)} %get-tuple-element.55), channel_id=1, source_target_pairs={{0,4},{4,8},{8,12},{12,16},{16,20},{20,24},{24,28},{28,0},{1,5},{5... | collective-permute-start | bytes 196616 | tf_op jit(solution)/shard_map/ppermute | solution.py:18
  13.9 2.1 copy-start.9
  13.9 2.4 %copy-start.8 = (f32[2,8,64,128]{3,2,1,0:T(8,128)S(1)}, f32[2,8,64,128]{3,2,1,0:T(8,128)}, u32[]{:S(2)}) copy-start(f32[2,8,64,128]{3,2,1,0:T(8,128)} %param.7) | copy-start | bytes 1572868
  13.9 2.4 %copy-start.10 = (f32[2,8,64,128]{3,2,1,0:T(8,128)S(1)}, f32[2,8,64,128]{3,2,1,0:T(8,128)}, u32[]{:S(2)}) copy-start(f32[2,8,64,128]{3,2,1,0:T(8,128)} %param.6) | copy-start | bytes 1572868
  16.3 42.2 %copy-start = (f32[8,64,128]{1,0,2:T(8,128)}, f32[8,64,128]{1,0,2:T(8,128)S(1)}, u32[]{:S(2)}) copy-start(f32[8,64,128]{1,0,2:T(8,128)S(1)} %copy.127) | copy-start | bytes 786436
  35.7 3.0 %copy-start.12 = (f32[8,64,128]{2,1,0:T(8,128)S(1)}, f32[8,64,128]{2,1,0:T(8,128)}, u32[]{:S(2)}) copy-start(f32[8,64,128]{2,1,0:T(8,128)} %param.9) | copy-start | bytes 786436
  36.0 22.5 %copy-start.3 = (f32[8,64,128]{1,0,2:T(8,128)}, f32[8,64,128]{1,0,2:T(8,128)S(1)}, u32[]{:S(2)}) copy-start(f32[8,64,128]{1,0,2:T(8,128)S(1)} %copy.129) | copy-start | bytes 786436
  46.9 5.9 %copy-start.20 = (f32[8]{0:T(128)S(1)}, f32[8]{0:T(128)}, u32[]{:S(2)}) copy-start(f32[8]{0:T(128)} %param.10) | copy-start | bytes 100
  46.9 5.9 %copy-start.21 = (s32[2]{0:T(128)S(1)}, s32[2]{0:T(128)}, u32[]{:S(2)}) copy-start(s32[2]{0:T(128)} %param.11) | copy-start | bytes 28
  53.0 79.9 %copy-start.14 = (f32[2]{0:T(128)}, f32[2]{0:T(128)S(1)}, u32[]{:S(2)}) copy-start(f32[2]{0:T(128)S(1)} %fusion.112) | copy-start | bytes 28
  53.0 5.6 %copy-start.18 = (f32[2,8,64,1]{2,1,3,0:T(8,128)S(1)}, f32[2,8,64,1]{2,1,3,0:T(8,128)}, u32[]{:S(2)}) copy-start(f32[2,8,64,1]{2,1,3,0:T(8,128)} %get-tuple-element.51) | copy-start | bytes 12292
  53.0 5.6 %copy-start.19 = (f32[2,8,64,1]{2,1,3,0:T(8,128)S(1)}, f32[2,8,64,1]{2,1,3,0:T(8,128)}, u32[]{:S(2)}) copy-start(f32[2,8,64,1]{2,1,3,0:T(8,128)} %get-tuple-element.52) | copy-start | bytes 12292
  64.1 8.3 %copy-start.1 = (f32[8,64,128]{1,0,2:T(8,128)S(1)}, f32[8,64,128]{1,0,2:T(8,128)}, u32[]{:S(2)}) copy-start(f32[8,64,128]{1,0,2:T(8,128)} %copy-done) | copy-start | bytes 786436
  64.1 8.3 %copy-start.4 = (f32[8,64,128]{1,0,2:T(8,128)S(1)}, f32[8,64,128]{1,0,2:T(8,128)}, u32[]{:S(2)}) copy-start(f32[8,64,128]{1,0,2:T(8,128)} %copy-done.3) | copy-start | bytes 786436
  64.4 5.2 %collective-permute-start.2 = (f32[2,1,64,128]{2,1,3,0:T(1,128)S(1)}, f32[2,1,64,128]{2,1,3,0:T(1,128)S(1)}, u32[]{:S(2)}, u32[]{:S(2)}) collective-permute-start(f32[2,1,64,128]{2,1,3,0:T(1,128)S(1)} %get-tuple-element.45), channel_id=1, source_target_pairs={{4,0},{8,4},{12,8},{16,12},{20,16},{24,20},{28,24},{0,28},{5,1},{9... | collective-permute-start | bytes 196616 | tf_op jit(solution)/shard_map/ppermute | solution.py:21
  67.1 5.3 %collective-permute-start.3 = (f32[2,1,64,128]{2,1,3,0:T(1,128)S(1)}, f32[2,1,64,128]{2,1,3,0:T(1,128)S(1)}, u32[]{:S(2)}, u32[]{:S(2)}) collective-permute-start(f32[2,1,64,128]{2,1,3,0:T(1,128)S(1)} %get-tuple-element.46), channel_id=1, source_target_pairs={{0,4},{4,8},{8,12},{12,16},{16,20},{20,24},{24,28},{28,0},{1,5},{5... | collective-permute-start | bytes 196616 | tf_op jit(solution)/shard_map/ppermute | solution.py:18
  74.8 3.8 %collective-permute-start.4 = (f32[2,1,64,128]{2,1,3,0:T(1,128)S(1)}, f32[2,1,64,128]{2,1,3,0:T(1,128)S(1)}, u32[]{:S(2)}, u32[]{:S(2)}) collective-permute-start(f32[2,1,64,128]{2,1,3,0:T(1,128)S(1)} %get-tuple-element.35), channel_id=1, source_target_pairs={{4,0},{8,4},{12,8},{16,12},{20,16},{24,20},{28,24},{0,28},{5,1},{9... | collective-permute-start | bytes 196616 | tf_op jit(solution)/shard_map/ppermute | solution.py:21
  74.9 5.5 %collective-permute-start.5 = (f32[2,1,64,128]{2,1,3,0:T(1,128)S(1)}, f32[2,1,64,128]{2,1,3,0:T(1,128)S(1)}, u32[]{:S(2)}, u32[]{:S(2)}) collective-permute-start(f32[2,1,64,128]{2,1,3,0:T(1,128)S(1)} %get-tuple-element.36), channel_id=1, source_target_pairs={{0,4},{4,8},{8,12},{12,16},{16,20},{20,24},{24,28},{28,0},{1,5},{5... | collective-permute-start | bytes 196616 | tf_op jit(solution)/shard_map/ppermute | solution.py:18
  133.0 10.8 %copy-start.15 = (f32[2]{0:T(128)S(1)}, f32[2]{0:T(128)}, u32[]{:S(2)}) copy-start(f32[2]{0:T(128)} %copy-done.14) | copy-start | bytes 28
  133.2 2.6 %collective-permute-start.6 = (f32[2,1,32,64]{3,2,1,0:T(8,128)S(1)}, f32[2,1,32,64]{3,2,1,0:T(8,128)S(1)}, u32[]{:S(2)}, u32[]{:S(2)}) collective-permute-start(f32[2,1,32,64]{3,2,1,0:T(8,128)S(1)} %get-tuple-element.97), channel_id=1, source_target_pairs={{4,0},{8,4},{12,8},{16,12},{20,16},{24,20},{28,24},{0,28},{5,1},{9... | collective-permute-start | bytes 49160 | tf_op jit(solution)/shard_map/ppermute | solution.py:21
  134.2 4.2 %collective-permute-start.7 = (f32[2,1,32,64]{3,2,1,0:T(8,128)S(1)}, f32[2,1,32,64]{3,2,1,0:T(8,128)S(1)}, u32[]{:S(2)}, u32[]{:S(2)}) collective-permute-start(f32[2,1,32,64]{3,2,1,0:T(8,128)S(1)} %get-tuple-element.98), channel_id=1, source_target_pairs={{0,4},{4,8},{8,12},{12,16},{16,20},{20,24},{24,28},{28,0},{1,5},{5... | collective-permute-start | bytes 49160 | tf_op jit(solution)/shard_map/ppermute | solution.py:18
  139.5 1.7 collective-permute-start.8
  139.6 4.3 %collective-permute-start.9 = (f32[2,1,32,64]{3,2,1,0:T(8,128)S(1)}, f32[2,1,32,64]{3,2,1,0:T(8,128)S(1)}, u32[]{:S(2)}, u32[]{:S(2)}) collective-permute-start(f32[2,1,32,64]{3,2,1,0:T(8,128)S(1)} %get-tuple-element.88), channel_id=1, source_target_pairs={{0,4},{4,8},{8,12},{12,16},{16,20},{20,24},{24,28},{28,0},{1,5},{5... | collective-permute-start | bytes 49160 | tf_op jit(solution)/shard_map/ppermute | solution.py:18
  154.4 15.8 %copy-start.11 = (f32[2,2,16,32]{3,2,1,0:T(8,128)S(1)}, f32[2,2,16,32]{3,2,1,0:T(8,128)}, u32[]{:S(2)}) copy-start(f32[2,2,16,32]{3,2,1,0:T(8,128)} %reduce_sum.57) | copy-start | bytes 24580
  154.4 15.8 %copy-start.13 = (f32[2,16,32]{2,1,0:T(8,128)S(1)}, f32[2,16,32]{2,1,0:T(8,128)}, u32[]{:S(2)}) copy-start(f32[2,16,32]{2,1,0:T(8,128)} %get-tuple-element.131) | copy-start | bytes 12292
  154.4 15.8 %copy-start.16 = (f32[2]{0:T(128)S(1)}, f32[2]{0:T(128)}, u32[]{:S(2)}) copy-start(f32[2]{0:T(128)} %copy-done.14) | copy-start | bytes 28
  155.5 1.6 collective-permute-start.10
  155.6 4.1 %collective-permute-start.11 = (f32[2,1,16,32]{3,2,1,0:T(8,128)S(1)}, f32[2,1,16,32]{3,2,1,0:T(8,128)S(1)}, u32[]{:S(2)}, u32[]{:S(2)}) collective-permute-start(f32[2,1,16,32]{3,2,1,0:T(8,128)S(1)} %get-tuple-element.130), channel_id=1, source_target_pairs={{0,4},{4,8},{8,12},{12,16},{16,20},{20,24},{24,28},{28,0},{1,5},{5... | collective-permute-start | bytes 12296 | tf_op jit(solution)/shard_map/ppermute | solution.py:18
  160.8 1.5 collective-permute-start.12
  160.8 4.1 %collective-permute-start.13 = (f32[2,1,16,32]{3,2,1,0:T(8,128)S(1)}, f32[2,1,16,32]{3,2,1,0:T(8,128)S(1)}, u32[]{:S(2)}, u32[]{:S(2)}) collective-permute-start(f32[2,1,16,32]{3,2,1,0:T(8,128)S(1)} %get-tuple-element.120), channel_id=1, source_target_pairs={{0,4},{4,8},{8,12},{12,16},{16,20},{20,24},{24,28},{28,0},{1,5},{5... | collective-permute-start | bytes 12296 | tf_op jit(solution)/shard_map/ppermute | solution.py:18
  166.0 1.5 collective-permute-start.14
  166.1 4.1 %collective-permute-start.15 = (f32[2,1,16,32]{3,2,1,0:T(8,128)S(1)}, f32[2,1,16,32]{3,2,1,0:T(8,128)S(1)}, u32[]{:S(2)}, u32[]{:S(2)}) collective-permute-start(f32[2,1,16,32]{3,2,1,0:T(8,128)S(1)} %get-tuple-element.110), channel_id=1, source_target_pairs={{0,4},{4,8},{8,12},{12,16},{16,20},{20,24},{24,28},{28,0},{1,5},{5... | collective-permute-start | bytes 12296 | tf_op jit(solution)/shard_map/ppermute | solution.py:18
  177.1 10.0 %copy-start.17 = (f32[2]{0:T(128)S(1)}, f32[2]{0:T(128)}, u32[]{:S(2)}) copy-start(f32[2]{0:T(128)} %copy-done.14) | copy-start | bytes 28
  177.3 1.7 collective-permute-start.16
  177.3 4.3 %collective-permute-start.17 = (f32[2,1,32,64]{3,2,1,0:T(8,128)S(1)}, f32[2,1,32,64]{3,2,1,0:T(8,128)S(1)}, u32[]{:S(2)}, u32[]{:S(2)}) collective-permute-start(f32[2,1,32,64]{3,2,1,0:T(8,128)S(1)} %get-tuple-element.78), channel_id=1, source_target_pairs={{0,4},{4,8},{8,12},{12,16},{16,20},{20,24},{24,28},{28,0},{1,5},{5... | collective-permute-start | bytes 49160 | tf_op jit(solution)/shard_map/ppermute | solution.py:18
  182.7 1.8 collective-permute-start.18
  182.9 4.2 %collective-permute-start.19 = (f32[2,1,32,64]{3,2,1,0:T(8,128)S(1)}, f32[2,1,32,64]{3,2,1,0:T(8,128)S(1)}, u32[]{:S(2)}, u32[]{:S(2)}) collective-permute-start(f32[2,1,32,64]{3,2,1,0:T(8,128)S(1)} %get-tuple-element.68), channel_id=1, source_target_pairs={{0,4},{4,8},{8,12},{12,16},{16,20},{20,24},{24,28},{28,0},{1,5},{5... | collective-permute-start | bytes 49160 | tf_op jit(solution)/shard_map/ppermute | solution.py:18
  192.1 3.8 %collective-permute-start.20 = (f32[2,1,64,128]{2,1,3,0:T(1,128)S(1)}, f32[2,1,64,128]{2,1,3,0:T(1,128)S(1)}, u32[]{:S(2)}, u32[]{:S(2)}) collective-permute-start(f32[2,1,64,128]{2,1,3,0:T(1,128)S(1)} %get-tuple-element.25), channel_id=1, source_target_pairs={{4,0},{8,4},{12,8},{16,12},{20,16},{24,20},{28,24},{0,28},{5,1},{9... | collective-permute-start | bytes 196616 | tf_op jit(solution)/shard_map/ppermute | solution.py:21
  192.2 5.3 %collective-permute-start.21 = (f32[2,1,64,128]{2,1,3,0:T(1,128)S(1)}, f32[2,1,64,128]{2,1,3,0:T(1,128)S(1)}, u32[]{:S(2)}, u32[]{:S(2)}) collective-permute-start(f32[2,1,64,128]{2,1,3,0:T(1,128)S(1)} %get-tuple-element.26), channel_id=1, source_target_pairs={{0,4},{4,8},{8,12},{12,16},{16,20},{20,24},{24,28},{28,0},{1,5},{5... | collective-permute-start | bytes 196616 | tf_op jit(solution)/shard_map/ppermute | solution.py:18
  192.8 4.7 %copy-start.2 = (f32[8,64,128]{1,0,2:T(8,128)S(1)}, f32[8,64,128]{1,0,2:T(8,128)}, u32[]{:S(2)}) copy-start(f32[8,64,128]{1,0,2:T(8,128)} %copy-done) | copy-start | bytes 786436
  192.8 4.7 %copy-start.5 = (f32[8,64,128]{1,0,2:T(8,128)S(1)}, f32[8,64,128]{1,0,2:T(8,128)}, u32[]{:S(2)}) copy-start(f32[8,64,128]{1,0,2:T(8,128)} %copy-done.3) | copy-start | bytes 786436
  199.1 4.2 %collective-permute-start.22 = (f32[2,1,64,128]{2,1,3,0:T(1,128)S(1)}, f32[2,1,64,128]{2,1,3,0:T(1,128)S(1)}, u32[]{:S(2)}, u32[]{:S(2)}) collective-permute-start(f32[2,1,64,128]{2,1,3,0:T(1,128)S(1)} %get-tuple-element.15), channel_id=1, source_target_pairs={{4,0},{8,4},{12,8},{16,12},{20,16},{24,20},{28,24},{0,28},{5,1},{9... | collective-permute-start | bytes 196616 | tf_op jit(solution)/shard_map/ppermute | solution.py:21
  200.6 5.3 %collective-permute-start.23 = (f32[2,1,64,128]{2,1,3,0:T(1,128)S(1)}, f32[2,1,64,128]{2,1,3,0:T(1,128)S(1)}, u32[]{:S(2)}, u32[]{:S(2)}) collective-permute-start(f32[2,1,64,128]{2,1,3,0:T(1,128)S(1)} %get-tuple-element.16), channel_id=1, source_target_pairs={{0,4},{4,8},{8,12},{12,16},{16,20},{20,24},{24,28},{28,0},{1,5},{5... | collective-permute-start | bytes 196616 | tf_op jit(solution)/shard_map/ppermute | solution.py:18
  208.2 1.7 copy-start.6
  210.3 14.6 %copy-start.7 = (f32[8,8,64,128]{3,2,1,0:T(8,128)S(1)}, f32[8,8,64,128]{3,2,1,0:T(8,128)}, u32[]{:S(2)}) copy-start(f32[8,8,64,128]{3,2,1,0:T(8,128)} %all-gather.4.cloned.1.call-done) | copy-start | bytes 6291460
Sparse Core Ops, SparseCore 0:
  11.0 47.1 all-gather.3
